TPU v7x, 32 devices: a whole 2x2x4 slice. The times are simulated.
32 devices in a mesh: group: 8 (over z, y), rep: 4 (over x, core).
Axes of the slice: x: 2, y: 2, z: 4, core: 2. Of those that a mesh axis runs over, the one named last changes fastest.
Arguments:
- grad_parts: bfloat16 [4, 24, 1024, 1024], P('rep', None, 'group'), may hold values from -40 to 40
- params: bfloat16 [24, 1024, 1024], P('rep', 'group'), may hold values from -6 to 6
- accum: float32 [24, 1024, 1024], P('rep', 'group'), may hold values from 1 to 50
- left_pre: bfloat16 [4, 8, 1, 1024, 1024], P('rep', 'group'), may hold values from -1 to 4
- right_pre: bfloat16 [4, 8, 1, 1024, 1024], P('rep', 'group'), may hold values from -1 to 4
- slot_block: int32 [4, 8, 1], replicated, may hold values from -1 to 5, as said below
- layer_of: int32 [24], replicated, may hold values from 0 to 7
Outputs:
- new_params: bfloat16 [24, 1024, 1024], P(None, 'group')
- new_accum: float32 [24, 1024, 1024], P('rep', 'group')
Inputs may be any that keep to these rules, and one draw needn't show every extreme that they name: For every replica q each of its 6 blocks is named by exactly one slot of slot_block[q]; a device's used slots come first and the others hold -1; in every replica some device has all 1 slots used.
All inputs are finite; a program needn't handle non-finite values.
Results may differ from a plain program's by a relative error of at most 0.018.
Values may be sent and summed in bfloat16 or wider, within the bound.
A program may use at most 128 MiB of HBM per device.

v0:
```python
import jax
import jax.numpy as jnp
from jax import lax
from jax.sharding import PartitionSpec as P

LAYERS = 8
step_rate = 0.5


def send_back(precond, group_size):
    slot_count = precond.shape[0]
    block_width = precond.shape[2]
    shard_rows = block_width // group_size
    spread = precond.reshape(1, slot_count, group_size, shard_rows, block_width)
    returned = lax.all_to_all(spread, "group", split_axis=2, concat_axis=0, tiled=True)
    return returned.reshape(group_size * slot_count, shard_rows, block_width)


def local(grad_parts, params, accum, left_pre, right_pre, slot_block, layer_of):
    group_size = lax.axis_size("group")
    replica_index = lax.axis_index("rep")
    group_index = lax.axis_index("group")
    blocks_rep = params.shape[0]
    shard_rows = params.shape[1]
    block_width = params.shape[2]
    slot_count = left_pre.shape[2]
    summed = lax.psum_scatter(
        grad_parts[0].astype(jnp.float32).astype(jnp.bfloat16),
        "rep",
        scatter_dimension=0,
        tiled=True,
    )
    gradient_wide = summed.astype(jnp.float32)
    new_accum = accum + gradient_wide * gradient_wide
    graft = gradient_wide * lax.rsqrt(new_accum)
    graft_blocks = jnp.sum(graft * graft, axis=(1, 2))
    my_layers = lax.dynamic_slice_in_dim(layer_of, replica_index * blocks_rep, blocks_rep)
    onehot_rep = (my_layers[:, None] == jnp.arange(LAYERS, dtype=jnp.int32)[None, :]).astype(
        jnp.float32
    )
    graft_layer = jnp.sum(onehot_rep * graft_blocks[:, None], axis=0)
    owner_table = lax.dynamic_index_in_dim(slot_block, replica_index, 0, keepdims=False)
    flat_table = owner_table.reshape(-1)
    slot_valid = flat_table >= 0
    picked = jnp.take(summed, jnp.maximum(flat_table, 0), axis=0)
    outgoing = jnp.where(slot_valid[:, None, None], picked, jnp.zeros_like(picked))
    outgoing = outgoing.reshape(group_size, slot_count, shard_rows, block_width)
    owned_blocks = lax.all_to_all(outgoing, "group", split_axis=0, concat_axis=2, tiled=True)[0]
    lefts = left_pre[0, 0]
    rights = right_pre[0, 0]
    left_product = jnp.einsum(
        "sij,sjk->sik", lefts, owned_blocks, preferred_element_type=jnp.float32
    ).astype(jnp.bfloat16)
    precond = jnp.einsum(
        "sij,sjk->sik", left_product, rights, preferred_element_type=jnp.float32
    ).astype(jnp.bfloat16)
    slot_total = flat_table.shape[0]
    position = jnp.sum(
        jnp.where(
            flat_table[None, :] == jnp.arange(blocks_rep, dtype=jnp.int32)[:, None],
            jnp.arange(slot_total, dtype=jnp.int32)[None, :],
            0,
        ),
        axis=1,
    )
    precond_wide = precond.astype(jnp.float32)
    slot_squares = jnp.sum(precond_wide * precond_wide, axis=(1, 2))
    my_slots = lax.dynamic_index_in_dim(owner_table, group_index, 0, keepdims=False)
    selected = (my_slots[:, None] == jnp.arange(blocks_rep, dtype=jnp.int32)[None, :]).astype(
        jnp.float32
    )
    slot_onehot = jnp.sum(selected[:, :, None] * onehot_rep[None, :, :], axis=1)
    shampoo_part = jnp.sum(slot_onehot * slot_squares[:, None], axis=0)
    graft_sq, shampoo_sq = lax.psum((graft_layer, shampoo_part), ("group", "rep"))
    returned = send_back(precond, group_size)
    precond_rows = jnp.take(returned, position, axis=0)
    layer_scale = jnp.sqrt(graft_sq) * lax.rsqrt(shampoo_sq + 1e-06)
    block_scale = jnp.sum(onehot_rep * layer_scale[None, :], axis=1)
    updated = (
        params.astype(jnp.float32)
        - step_rate * block_scale[:, None, None] * precond_rows.astype(jnp.float32)
    ).astype(jnp.bfloat16)
    new_params = lax.all_gather(updated, "rep", axis=0, tiled=True)
    return (new_params, new_accum)


def solution(mesh):
    in_specs = (
        P("rep", None, "group", None),
        P("rep", "group", None),
        P("rep", "group", None),
        P("rep", "group", None, None, None),
        P("rep", "group", None, None, None),
        P(),
        P(),
    )
    out_specs = (P(None, "group", None), P("rep", "group", None))
    return jax.shard_map(local, mesh=mesh, in_specs=in_specs, out_specs=out_specs, check_vma=False)
```

profile of v0, /device:TPU:0, one launch (start us, length us, event | category | flops | bytes accessed | tf_op | source)
XLA Modules:
  0.0 279.0 jit_solution(11084299918333157456)
XLA Ops:
  7.2 0.0 copy-start
  7.2 0.0 reduce-scatter.2.cloned.1.call-start
  7.2 0.0 copy-start.1
  7.2 0.7 reduce-scatter.2.cloned.1.call-update
  7.9 0.1 copy-done.1
  8.1 64.1 %reduce-scatter.2.cloned.1.call-done = bf16[6,128,1024]{2,1,0:T(8,128)(2,1)} async-done(((bf16[24,128,1024]{2,1,0:T(8,128)(2,1)}), bf16[6,128,1024]{2,1,0:T(8,128)(2,1)}) %reduce-scatter.2.cloned.1.call-update) | async-done | bytes 1572880 | tf_op jit(solution)/shard_map/reduce_scatter | solution.py:27
  72.1 3.4 %gather_fusion = bf16[8,128,1024]{2,1,0:T(8,128)(2,1)} fusion(bf16[6,128,1024]{2,1,0:T(8,128)(2,1)} %reduce-scatter.2.cloned.1.call-done, s32[1024]{0:T(1024)S(1)} %pad_clamp_fusion.1), kind=kCustom, calls=%fused_computation | custom fusion | bytes 4194336 | tf_op jit(solution)/shard_map/jit(_take)/gather | solution.py:45
  75.5 1.9 fusion.7
  77.4 53.5 %all_to_all.8 = bf16[8,1,128,1024]{3,2,1,0:T(8,128)(2,1)} all-to-all(bf16[8,1,128,1024]{3,2,1,0:T(8,128)(2,1)S(1)} %fusion.7), channel_id=1, replica_groups=mesh['group'=8,'rep'=4] {'group'}, dimensions={0} | all-to-all | bytes 4194304 | tf_op jit(solution)/shard_map/all_to_all | solution.py:48
  130.9 0.0 copy-done
  130.9 8.8 %multiply_reduce_fusion = (f32[]{:T(128)}, bf16[1024,1024]{1,0:T(8,128)(2,1)}) fusion(bf16[1,1,1,1024,1024]{4,3,2,1,0:T(8,128)(2,1)S(1)} %copy-done, bf16[1024,1024]{1,0:T(8,128)(2,1)} %bitcast.39, bf16[1,1,1,1024,1024]{4,3,2,1,0:T(8,128)(2,1)} %param.10), kind=kOutput, calls=%fused_computation.2 | convolution fusion | flops 4300210176 | bytes 8388612 | tf_op jit(solution)/shard_map/sij,sjk->sik/dot_general | solution.py:54
  139.8 0.0 copy-start.2
  139.8 4.5 %all-to-all-start.1 = ((bf16[1,1,8,128,1024]{4,3,1,0,2:T(8,128)(2,1)}), bf16[1,1,8,128,1024]{4,3,1,0,2:T(8,128)(2,1)}, u32[]{:S(2)}, u32[]{:S(2)}) async-start(bf16[1,1,8,128,1024]{4,3,1,0,2:T(8,128)(2,1)} %bitcast.38), calls=%async_computation.2 | async-start | bytes 4194304 | tf_op jit(solution)/shard_map/all_to_all | solution.py:15
  144.2 0.0 all-gather.2.cloned.1.call-start
  144.3 0.6 constant_dynamic-slice_fusion.1
  144.9 0.0 copy-done.2
  144.9 0.1 dynamic_slice.11
  145.0 0.6 compare_convert_fusion
  145.6 0.1 select_reduce_fusion
  145.7 0.1 fusion.18
  145.9 4.7 %fusion.2 = (f32[6]{0:T(128)S(1)}, f32[6,128,1024]{2,1,0:T(8,128)}) fusion(bf16[6,128,1024]{2,1,0:T(8,128)(2,1)} %reduce-scatter.2.cloned.1.call-done, f32[6,128,1024]{2,1,0:T(8,128)} %param.9), kind=kLoop, calls=%fused_computation.7 | loop fusion | flops 4718586 | bytes 7864344 | tf_op jit(solution)/shard_map/reduce_sum | solution.py:36
  150.6 0.1 select_reduce_fusion.2
  150.7 0.6 broadcast_multiply_fusion.1
  151.3 59.8 %all-reduce = (f32[8]{0:T(128)S(1)}, f32[8]{0:T(128)S(1)}) all-reduce(f32[8]{0:T(128)S(1)} %broadcast_multiply_fusion.1, f32[8]{0:T(128)S(1)} %select_reduce_fusion.2), channel_id=1, replica_groups=mesh['group'=8,'rep'=4] {'group','rep'}, use_global_device_ids=true, to_apply=%region_6.7 | all-reduce | flops 16 | bytes 128 | tf_op jit(solution)/shard_map/psum | solution.py:74
  211.1 0.2 select_reduce_fusion.1
  211.2 0.0 all-to-all-done.1
  211.3 3.4 %gather_fusion.1 = bf16[6,128,1024]{2,1,0:T(8,128)(2,1)} fusion(bf16[8,128,1024]{2,1,0:T(8,128)(2,1)} %bitcast.10, s32[1024]{0:T(1024)S(1)} %pad_clamp_fusion), kind=kCustom, calls=%fused_computation.1 | custom fusion | bytes 3145752 | tf_op jit(solution)/shard_map/jit(_take)/gather | solution.py:76
  214.7 4.0 %subtract_convert_fusion = bf16[6,128,1024]{2,1,0:T(8,128)(2,1)} fusion(bf16[6,128,1024]{2,1,0:T(8,128)(2,1)} %param.8, bf16[6,128,1024]{2,1,0:T(8,128)(2,1)} %gather_fusion.1, f32[6]{0:T(128)S(1)} %broadcast_multiply_fusion, pred[6]{0:T(512)(128)(4,1)S(1)} %compare_and_fusion), kind=kLoop, calls=%fused_computation.8 | loop fusion | flops 4718592 | bytes 4718622 | tf_op jit(solution)/shard_map/convert_element_type | solution.py:82
  218.6 0.0 all-gather.2.cloned.1.call-update
  218.7 47.0 %all-gather.2.cloned.1.call-done = bf16[24,128,1024]{2,1,0:T(8,128)(2,1)} async-done(((bf16[6,128,1024]{2,1,0:T(8,128)(2,1)}), bf16[24,128,1024]{2,1,0:T(8,128)(2,1)}) %all-gather.2.cloned.1.call-update) | async-done | bytes 6291472 | tf_op jit(solution)/shard_map/all_gather | solution.py:83
  265.6 6.6 %copy.12 = bf16[24,128,1024]{2,1,0:T(8,128)(2,1)} copy(bf16[24,128,1024]{2,1,0:T(8,128)(2,1)} %all-gather.2.cloned.1.call-done) | data formatting | bytes 12582912
  (9 shorter events, 0.1 us)
Async XLA Ops:
  7.2 123.8 %copy-start = (bf16[1,1,1,1024,1024]{4,3,2,1,0:T(8,128)(2,1)S(1)}, bf16[1,1,1,1024,1024]{4,3,2,1,0:T(8,128)(2,1)}, u32[]{:S(2)}) copy-start(bf16[1,1,1,1024,1024]{4,3,2,1,0:T(8,128)(2,1)} %param.11) | copy-start | bytes 6291460
  7.2 65.0 %reduce-scatter.2.cloned.1.call-start = ((), (), s32[]{:S(2)}) async-start(), calls=%async_computation.3 | async-start | bytes 7864320 | tf_op jit(solution)/shard_map/reduce_scatter | solution.py:27
  7.2 0.8 copy-start.1
  139.8 5.1 %copy-start.2 = (s32[24]{0:T(128)S(1)}, s32[24]{0:T(128)}, u32[]{:S(2)}) copy-start(s32[24]{0:T(128)} %param.13) | copy-start | bytes 292
  139.8 71.5 %all-to-all-start.1 = ((bf16[1,1,8,128,1024]{4,3,1,0,2:T(8,128)(2,1)}), bf16[1,1,8,128,1024]{4,3,1,0,2:T(8,128)(2,1)}, u32[]{:S(2)}, u32[]{:S(2)}) async-start(bf16[1,1,8,128,1024]{4,3,1,0,2:T(8,128)(2,1)} %bitcast.38), calls=%async_computation.2 | async-start | bytes 4194304 | tf_op jit(solution)/shard_map/all_to_all | solution.py:15
  144.2 121.4 %all-gather.2.cloned.1.call-start = ((), (), s32[]{:S(2)}) async-start(), calls=%async_computation.4 | async-start | bytes 7864320 | tf_op jit(solution)/shard_map/all_gather | solution.py:83
Sparse Core Ops, SparseCore 0:
  10.5 61.5 reduce-scatter.1
  218.8 46.8 all-gather.1
where the time goes:
time: 280 us; the launch traced here: 279 us
  blocking collectives  113 us (40%)
  waiting for transfers between devices  112 us (40%)
  local copies, waits for them, and re-layouts  14.2 us (5%)
  between operations  14.1 us (5%)
  other arithmetic  12.3 us (4%)
  matrix products  8.83 us (3%)
  starting transfers between devices  4.55 us (2%)
    reduce_scatter x1, waiting for transfers between devices, local(): lax.psum_scatter(grad_parts[0].astype(jnp.float32).astype(jnp.bfloat16),...  64.1 us
    psum x1, blocking collectives, local(): lax.psum((graft_layer, shampoo_part), ('group', 'rep'))  59.8 us
    all_to_all x1, blocking collectives, local(): lax.all_to_all(outgoing, 'group', split_axis=0, concat_axis=2, tiled=True)  53.5 us
    all_gather x1, waiting for transfers between devices, local(): new_params = lax.all_gather(updated, 'rep', axis=0, tiled=True)  47 us
    dot_general x1, matrix products, local(): jnp.einsum('sij,sjk->sik', left_product, rights, preferred_element_type=j...  8.83 us
    unnamed x7, local copies, waits for them, and re-layouts  6.71 us
  transfers between devices with their start and end apart: 3, of which 2 were waited for; matrix products, arithmetic and copies ran while one was open for 3% of the time, Pallas kernels for 0%

commit v1 on v0

--- a/solution.py
+++ b/solution.py
@@ -71,7 +71,7 @@
     )
     slot_onehot = jnp.sum(selected[:, :, None] * onehot_rep[None, :, :], axis=1)
     shampoo_part = jnp.sum(slot_onehot * slot_squares[:, None], axis=0)
-    graft_sq, shampoo_sq = lax.psum((graft_layer, shampoo_part), ("group", "rep"))
+    graft_sq, shampoo_sq = lax.psum(lax.psum((graft_layer, shampoo_part), "rep"), "group")
     returned = send_back(precond, group_size)
     precond_rows = jnp.take(returned, position, axis=0)
     layer_scale = jnp.sqrt(graft_sq) * lax.rsqrt(shampoo_sq + 1e-06)

time: 280 us -> 266 us (0.950)
  blocking collectives: 113 us -> 94.7 us
  waiting for transfers between devices: 112 us -> 117 us
    psum x1 -> x2, blocking collectives: 59.8 us -> 41.3 us  [the longest x1 35.2 us: local(): lax.psum(lax.psum((graft_layer, shampoo_part), 'rep'), 'group')]
    all_gather x1, waiting for transfers between devices: 47 us -> 52 us  [local(): new_params = lax.all_gather(updated, 'rep', axis=0, tiled=True)]
where the time goes in v1:
time: 266 us
  waiting for transfers between devices  117 us (44%)
  blocking collectives  94.7 us (36%)
  local copies, waits for them, and re-layouts  14.2 us (5%)
  between operations  14.2 us (5%)
  other arithmetic  12.3 us (5%)
  matrix products  8.83 us (3%)
  starting transfers between devices  4.55 us (2%)
    reduce_scatter x1, waiting for transfers between devices, local(): lax.psum_scatter(grad_parts[0].astype(jnp.float32).astype(jnp.bfloat16),...  64.1 us
    all_to_all x1, blocking collectives, local(): lax.all_to_all(outgoing, 'group', split_axis=0, concat_axis=2, tiled=True)  53.5 us
    all_gather x1, waiting for transfers between devices, local(): new_params = lax.all_gather(updated, 'rep', axis=0, tiled=True)  52 us
    psum x1, blocking collectives, local(): lax.psum(lax.psum((graft_layer, shampoo_part), 'rep'), 'group')  35.2 us
    dot_general x1, matrix products, local(): jnp.einsum('sij,sjk->sik', left_product, rights, preferred_element_type=j...  8.83 us
    unnamed x7, local copies, waits for them, and re-layouts  6.71 us
    psum x1, blocking collectives, local(): lax.psum((graft_layer, shampoo_part), 'rep')  6.07 us
  transfers between devices with their start and end apart: 3, of which 2 were waited for; matrix products, arithmetic and copies ran while one was open for 3% of the time, Pallas kernels for 0%

profile of v1, /device:TPU:0, one launch (start us, length us, event | category | flops | bytes accessed | tf_op | source)
XLA Modules:
  0.0 265.6 jit_solution(436988168730412404)
XLA Ops:
  7.2 0.0 copy-start
  7.2 0.0 reduce-scatter.2.cloned.1.call-start
  7.2 0.0 copy-start.1
  7.2 0.7 reduce-scatter.2.cloned.1.call-update
  7.9 0.1 copy-done.1
  8.1 64.1 %reduce-scatter.2.cloned.1.call-done = bf16[6,128,1024]{2,1,0:T(8,128)(2,1)} async-done(((bf16[24,128,1024]{2,1,0:T(8,128)(2,1)}), bf16[6,128,1024]{2,1,0:T(8,128)(2,1)}) %reduce-scatter.2.cloned.1.call-update) | async-done | bytes 1572880 | tf_op jit(solution)/shard_map/reduce_scatter | solution.py:27
  72.1 3.4 %gather_fusion = bf16[8,128,1024]{2,1,0:T(8,128)(2,1)} fusion(bf16[6,128,1024]{2,1,0:T(8,128)(2,1)} %reduce-scatter.2.cloned.1.call-done, s32[1024]{0:T(1024)S(1)} %pad_clamp_fusion.1), kind=kCustom, calls=%fused_computation | custom fusion | bytes 4194336 | tf_op jit(solution)/shard_map/jit(_take)/gather | solution.py:45
  75.5 1.9 fusion.7
  77.4 53.5 %all_to_all.8 = bf16[8,1,128,1024]{3,2,1,0:T(8,128)(2,1)} all-to-all(bf16[8,1,128,1024]{3,2,1,0:T(8,128)(2,1)S(1)} %fusion.7), channel_id=1, replica_groups=mesh['group'=8,'rep'=4] {'group'}, dimensions={0} | all-to-all | bytes 4194304 | tf_op jit(solution)/shard_map/all_to_all | solution.py:48
  130.9 0.0 copy-done
  130.9 8.8 %multiply_reduce_fusion = (f32[]{:T(128)}, bf16[1024,1024]{1,0:T(8,128)(2,1)}) fusion(bf16[1,1,1,1024,1024]{4,3,2,1,0:T(8,128)(2,1)S(1)} %copy-done, bf16[1024,1024]{1,0:T(8,128)(2,1)} %bitcast.39, bf16[1,1,1,1024,1024]{4,3,2,1,0:T(8,128)(2,1)} %param.10), kind=kOutput, calls=%fused_computation.2 | convolution fusion | flops 4300210176 | bytes 8388612 | tf_op jit(solution)/shard_map/sij,sjk->sik/dot_general | solution.py:54
  139.8 0.0 copy-start.2
  139.8 4.5 %all-to-all-start.1 = ((bf16[1,1,8,128,1024]{4,3,1,0,2:T(8,128)(2,1)}), bf16[1,1,8,128,1024]{4,3,1,0,2:T(8,128)(2,1)}, u32[]{:S(2)}, u32[]{:S(2)}) async-start(bf16[1,1,8,128,1024]{4,3,1,0,2:T(8,128)(2,1)} %bitcast.38), calls=%async_computation.2 | async-start | bytes 4194304 | tf_op jit(solution)/shard_map/all_to_all | solution.py:15
  144.2 0.0 all-gather.2.cloned.1.call-start
  144.3 0.6 constant_dynamic-slice_fusion.1
  144.9 0.0 copy-done.2
  144.9 0.1 dynamic_slice.11
  145.0 0.6 compare_convert_fusion
  145.6 0.1 select_reduce_fusion
  145.7 0.1 fusion.18
  145.9 4.7 %fusion.2 = (f32[6]{0:T(128)S(1)}, f32[6,128,1024]{2,1,0:T(8,128)}) fusion(bf16[6,128,1024]{2,1,0:T(8,128)(2,1)} %reduce-scatter.2.cloned.1.call-done, f32[6,128,1024]{2,1,0:T(8,128)} %param.9), kind=kLoop, calls=%fused_computation.7 | loop fusion | flops 4718586 | bytes 7864344 | tf_op jit(solution)/shard_map/reduce_sum | solution.py:36
  150.6 0.1 select_reduce_fusion.2
  150.7 0.6 broadcast_multiply_fusion.1
  151.3 6.1 %all-reduce.1 = (f32[8]{0:T(128)S(1)}, f32[8]{0:T(128)S(1)}) all-reduce(f32[8]{0:T(128)S(1)} %broadcast_multiply_fusion.1, f32[8]{0:T(128)S(1)} %select_reduce_fusion.2), channel_id=1, replica_groups=mesh['group'=8,'rep'=4] {'rep'}, use_global_device_ids=true, to_apply=%region_7.8 | all-reduce | flops 16 | bytes 128 | tf_op jit(solution)/shard_map/psum | solution.py:74
  157.3 35.2 %all-reduce = (f32[8]{0:T(128)S(1)}, f32[8]{0:T(128)S(1)}) all-reduce(f32[8]{0:T(128)S(1)} %get-tuple-element.4, f32[8]{0:T(128)S(1)} %get-tuple-element.5), channel_id=1, replica_groups=mesh['group'=8,'rep'=4] {'group'}, use_global_device_ids=true, to_apply=%region_8.9 | all-reduce | flops 16 | bytes 128 | tf_op jit(solution)/shard_map/psum | solution.py:74
  192.5 0.2 select_reduce_fusion.1
  192.7 0.0 all-to-all-done.1
  192.7 3.4 %gather_fusion.1 = bf16[6,128,1024]{2,1,0:T(8,128)(2,1)} fusion(bf16[8,128,1024]{2,1,0:T(8,128)(2,1)} %bitcast.10, s32[1024]{0:T(1024)S(1)} %pad_clamp_fusion), kind=kCustom, calls=%fused_computation.1 | custom fusion | bytes 3145752 | tf_op jit(solution)/shard_map/jit(_take)/gather | solution.py:76
  196.2 4.0 %subtract_convert_fusion = bf16[6,128,1024]{2,1,0:T(8,128)(2,1)} fusion(bf16[6,128,1024]{2,1,0:T(8,128)(2,1)} %param.8, bf16[6,128,1024]{2,1,0:T(8,128)(2,1)} %gather_fusion.1, f32[6]{0:T(128)S(1)} %broadcast_multiply_fusion, pred[6]{0:T(512)(128)(4,1)S(1)} %compare_and_fusion), kind=kLoop, calls=%fused_computation.8 | loop fusion | flops 4718592 | bytes 4718622 | tf_op jit(solution)/shard_map/convert_element_type | solution.py:82
  200.1 0.0 all-gather.2.cloned.1.call-update
  200.1 52.0 %all-gather.2.cloned.1.call-done = bf16[24,128,1024]{2,1,0:T(8,128)(2,1)} async-done(((bf16[6,128,1024]{2,1,0:T(8,128)(2,1)}), bf16[24,128,1024]{2,1,0:T(8,128)(2,1)}) %all-gather.2.cloned.1.call-update) | async-done | bytes 6291472 | tf_op jit(solution)/shard_map/all_gather | solution.py:83
  252.2 6.6 %copy.12 = bf16[24,128,1024]{2,1,0:T(8,128)(2,1)} copy(bf16[24,128,1024]{2,1,0:T(8,128)(2,1)} %all-gather.2.cloned.1.call-done) | data formatting | bytes 12582912
  (9 shorter events, 0.1 us)
Async XLA Ops:
  7.2 123.8 %copy-start = (bf16[1,1,1,1024,1024]{4,3,2,1,0:T(8,128)(2,1)S(1)}, bf16[1,1,1,1024,1024]{4,3,2,1,0:T(8,128)(2,1)}, u32[]{:S(2)}) copy-start(bf16[1,1,1,1024,1024]{4,3,2,1,0:T(8,128)(2,1)} %param.11) | copy-start | bytes 6291460
  7.2 65.0 %reduce-scatter.2.cloned.1.call-start = ((), (), s32[]{:S(2)}) async-start(), calls=%async_computation.3 | async-start | bytes 7864320 | tf_op jit(solution)/shard_map/reduce_scatter | solution.py:27
  7.2 0.8 copy-start.1
  139.8 5.1 %copy-start.2 = (s32[24]{0:T(128)S(1)}, s32[24]{0:T(128)}, u32[]{:S(2)}) copy-start(s32[24]{0:T(128)} %param.13) | copy-start | bytes 292
  139.8 53.0 %all-to-all-start.1 = ((bf16[1,1,8,128,1024]{4,3,1,0,2:T(8,128)(2,1)}), bf16[1,1,8,128,1024]{4,3,1,0,2:T(8,128)(2,1)}, u32[]{:S(2)}, u32[]{:S(2)}) async-start(bf16[1,1,8,128,1024]{4,3,1,0,2:T(8,128)(2,1)} %bitcast.38), calls=%async_computation.2 | async-start | bytes 4194304 | tf_op jit(solution)/shard_map/all_to_all | solution.py:15
  144.2 107.9 %all-gather.2.cloned.1.call-start = ((), (), s32[]{:S(2)}) async-start(), calls=%async_computation.4 | async-start | bytes 7864320 | tf_op jit(solution)/shard_map/all_gather | solution.py:83
Sparse Core Ops, SparseCore 0:
  10.5 61.5 reduce-scatter.1
  200.3 51.8 all-gather.1
